TPU v7x, 32 devices: a whole 2x2x4 slice. The times are simulated.
32 devices in a mesh: au: 4 (over y, x), vert: 8 (over z, core).
Axes of the slice: x: 2, y: 2, z: 4, core: 2. Of those that a mesh axis runs over, the one named last changes fastest.
Arguments:
- visibility: bfloat16 [2, 65536], P(None, ('au', 'vert')), may hold values from -6 to 6
- taps_u: bfloat16 [16, 65536], P(None, ('au', 'vert')), may hold values from 0.019897461 to 0.44921875
- taps_v: bfloat16 [16, 65536], P(None, ('au', 'vert')), may hold values from 0.019897461 to 0.44921875
- facet: int32 [65536, 1], P(('au', 'vert')), may hold values from 0 to 31; in each aligned block of 2048 rows (0 to 2047, 2048 to 4095, ...) at most 256 rows name the same one
- u_offset: int32 [65536], P(('au', 'vert')), may hold values from 0 to 2032
- v_offset: int32 [65536], P(('au', 'vert')), may hold values from 0 to 1008
Outputs:
- image: float32 [2, 8192, 8192], P(None, ('au', 'vert'))
Inputs may be any that keep to these rules, and one draw needn't show every extreme that they name: Of the 2048 visibilities of one device at most 256 name the same facet, and some facet gets exactly 256 of some device's visibilities.
All inputs are finite; a program needn't handle non-finite values.
Results may differ from a plain program's by a relative error of at most 0.0058.
Values may be sent and summed in bfloat16 or wider, within the bound.
A program may use at most 128 MiB of HBM per device.

v0:
```python
import functools
import math

import jax
import jax.numpy as jnp
from jax import lax
from jax.experimental import pallas as pl
from jax.experimental.pallas import tpu as pltpu
from jax.sharding import PartitionSpec as P

GRID = 8192
TAPS = 16
LANES = 128
LOW = 64
STEP_BLOCKS = 2
FIELDS = 40
ROWS_OUT = 8


def phase_table(left, right, modulus):
    product = left[:, None] * right[None, :] % modulus
    angle = product.astype(jnp.float32) * (2.0 * math.pi / modulus)
    return jnp.cos(angle), jnp.sin(angle)


def rotated(taps, shift):
    tap = jnp.arange(TAPS, dtype=jnp.int32)[:, None]
    turned = jnp.zeros_like(taps)
    for t in range(TAPS):
        turned = turned + jnp.where((shift[None, :] + t) % TAPS == tap, taps[t : t + 1], 0)
    return turned


def tile_spread_kernel(first_ref, last_ref, pay_ref, low_ref, high_ref, acc_ref, *, tile, tiles, rows, period):
    source = pl.program_id(0)

    @pl.when(source == 0)
    def _():
        def clear(n, carry):
            acc_ref[n] = jnp.zeros(acc_ref.shape[1:], jnp.float32)
            return carry

        lax.fori_loop(0, acc_ref.shape[0], clear, 0)

    tap = lax.broadcasted_iota(jnp.int32, (TAPS, tile), 0).astype(jnp.float32)
    step_cells = STEP_BLOCKS * LANES

    def one_tile(t, carry):
        lanes = pl.ds(pl.multiple_of(t * tile, tile), tile)
        taps_v = pay_ref[0, 0:TAPS, lanes]
        taps_u = pay_ref[0, TAPS : 2 * TAPS, lanes]
        extra = pay_ref[0, 2 * TAPS : 2 * TAPS + 8, lanes].astype(jnp.float32)
        col_sixteenth = extra[0:1] * 16.0 + extra[1:2]
        col_low = extra[2:3]
        row_high = extra[3:4].astype(jnp.bfloat16)
        row_sixteenth = extra[4:5]
        row_low = extra[5:6]
        vis_re = extra[6:7].astype(jnp.bfloat16)
        vis_im = extra[7:8].astype(jnp.bfloat16)
        zero = jnp.zeros((), jnp.bfloat16)
        spot_u = (row_sixteenth + jnp.where(tap < row_low, 1.0, 0.0)).astype(jnp.bfloat16)
        band_u = jnp.concatenate(
            [jnp.where(spot_u == jnp.bfloat16(q), taps_u, zero) for q in range(LOW // TAPS + 1)], axis=0
        )
        low = jnp.dot(low_ref[...], band_u, preferred_element_type=jnp.float32)
        high_count = GRID // LOW
        number = lax.broadcasted_iota(jnp.int32, (high_count, tile), 0).astype(jnp.float32).astype(jnp.bfloat16)
        here = number == jnp.broadcast_to(row_high, (high_count, tile))
        picked = jnp.concatenate(
            [
                jnp.where(here, jnp.broadcast_to(vis_re, (high_count, tile)), zero),
                jnp.where(here, jnp.broadcast_to(vis_im, (high_count, tile)), zero),
            ],
            axis=0,
        )
        high = jnp.dot(high_ref[...], picked, preferred_element_type=jnp.float32)
        high_re, high_im = high[:period], high[period:]
        parts_re, parts_im = [], []
        for begin in range(0, rows, period):
            low_re = low[begin : begin + period]
            low_im = low[rows + begin : rows + begin + period]
            parts_re.append((low_re * high_re - low_im * high_im).astype(jnp.bfloat16))
            parts_im.append((low_re * high_im + low_im * high_re).astype(jnp.bfloat16))
        spread = jnp.concatenate(parts_re + parts_im, axis=0)
        spot_v = col_sixteenth + jnp.where(tap < col_low, 1.0, 0.0)

        def one_step(block, carry):
            base = (block * (step_cells // TAPS)).astype(jnp.float32)
            near = jnp.clip(spot_v - base, -1.0, step_cells / TAPS).astype(jnp.bfloat16)
            band_v = jnp.concatenate(
                [jnp.where(near == jnp.bfloat16(q), taps_v, zero) for q in range(step_cells // TAPS)], axis=0
            )
            out = lax.dot_general(spread, band_v, (((1,), (1,)), ((), ())), preferred_element_type=jnp.float32)
            for j in range(STEP_BLOCKS):
                acc_ref[block * STEP_BLOCKS + j] += out[:, j * LANES : (j + 1) * LANES]
            return carry

        place = source * tiles + t
        lax.fori_loop(first_ref[place], last_ref[place] + 1, one_step, 0)
        return carry

    lax.fori_loop(0, tiles, one_tile, 0)


def row_transform_kernel(plane_ref, first_ref, cos_ref, sin_ref, second_ref, out_ref):
    length = plane_ref.shape[0]
    stack = jnp.concatenate(
        [
            jnp.concatenate([plane_ref[:, part, m, :] for m in range(ROWS_OUT)], axis=1)
            for part in range(2)
        ],
        axis=0,
    ).astype(jnp.bfloat16)
    mid = jnp.dot(first_ref[...], stack, preferred_element_type=jnp.float32)
    cos, sin = cos_ref[...], sin_ref[...]
    rows = []
    for m in range(ROWS_OUT):
        re = mid[:length, m * LANES : (m + 1) * LANES]
        im = mid[length:, m * LANES : (m + 1) * LANES]
        rows.append(
            jnp.concatenate(
                [(re * cos - im * sin).astype(jnp.bfloat16), (re * sin + im * cos).astype(jnp.bfloat16)], axis=1
            )
        )
    turned = jnp.concatenate(rows, axis=0)
    out = lax.dot_general(second_ref[...], turned, (((1,), (1,)), ((), ())), preferred_element_type=jnp.float32)
    half = LANES // 2
    left = lax.broadcasted_iota(jnp.int32, (half, LANES), 1) < half
    for part in range(2):
        for pair in range(ROWS_OUT // 2):
            lanes = slice(pair * LANES, (pair + 1) * LANES)
            even = out[2 * part * half : (2 * part + 1) * half, lanes]
            odd = out[(2 * part + 1) * half : (2 * part + 2) * half, lanes]
            out_ref[part, 2 * pair] = jnp.where(left, even, pltpu.roll(odd, half, 1))
            out_ref[part, 2 * pair + 1] = jnp.where(left, pltpu.roll(even, half, 1), odd)


def stacked(cos, sin):
    return jnp.concatenate(
        [jnp.concatenate([cos, -sin], axis=1), jnp.concatenate([sin, cos], axis=1)], axis=0
    ).astype(jnp.bfloat16)


def on_device(visibility, taps_u, taps_v, facet, u_offset, v_offset):
    n_au = lax.axis_size("au")
    n_vert = lax.axis_size("vert")
    devices = n_au * n_vert
    count = visibility.shape[1]
    rows = GRID // devices
    own = lax.axis_index("au") * n_vert + lax.axis_index("vert")
    target = facet[:, 0]
    row = target // n_vert * (GRID // n_au) + u_offset
    col = target % n_vert * (GRID // n_vert) + v_offset
    here = lax.axis_index("au")
    key = col * (n_au * count) + here * count + jnp.arange(count, dtype=jnp.int32)
    keys = lax.all_gather(key, "au", axis=0, tiled=True)
    rank = jnp.sum((keys[:, None] < key[None, :]).astype(jnp.int32), axis=0)
    scalars = jnp.stack(
        [col // 256, col % 256 // TAPS, col % TAPS, row // LOW, row % LOW // TAPS, row % TAPS]
    ).astype(jnp.bfloat16)
    ranks = jnp.stack([rank // 256, rank % 256]).astype(jnp.bfloat16)
    payload = jnp.concatenate(
        [rotated(taps_v, col % TAPS), rotated(taps_u, row % TAPS), scalars, visibility, ranks], axis=0
    )
    group = lax.all_gather(payload, "au", axis=1, tiled=True)
    places = group[FIELDS:].astype(jnp.int32)
    slot = places[0] * 256 + places[1] - here * count
    order = (slot[:, None] == jnp.arange(count, dtype=jnp.int32)[None, :]).astype(jnp.bfloat16)
    payload = jnp.dot(group[:FIELDS], order, preferred_element_type=jnp.float32).astype(jnp.bfloat16)
    gathered = lax.all_gather(payload, ("au", "vert"), axis=0)
    tile = math.gcd(count, 256)
    tiles = count // tile
    ends = gathered[:, 2 * TAPS : 2 * TAPS + 3, :].astype(jnp.int32)
    columns = (ends[:, 0] * 256 + ends[:, 1] * TAPS + ends[:, 2]).reshape(devices * tiles, tile)
    step_cells = STEP_BLOCKS * LANES
    first = jnp.min(columns, axis=1) // step_cells
    last = (jnp.max(columns, axis=1) + TAPS - 1) // step_cells

    k = own * rows + jnp.arange(rows, dtype=jnp.int32)
    low_cos, low_sin = phase_table(k, jnp.arange(LOW + TAPS, dtype=jnp.int32), GRID)
    low_table = jnp.concatenate([low_cos, low_sin], axis=0).astype(jnp.bfloat16)
    high_count = GRID // LOW
    period = min(rows, high_count)
    high_table = stacked(*phase_table(k[:period], jnp.arange(high_count, dtype=jnp.int32), high_count))
    blocks = GRID // LANES
    plane = pl.pallas_call(
        functools.partial(tile_spread_kernel, tile=tile, tiles=tiles, rows=rows, period=period),
        grid_spec=pltpu.PrefetchScalarGridSpec(
            num_scalar_prefetch=2,
            grid=(devices,),
            in_specs=[
                pl.BlockSpec((1, FIELDS, count), lambda s, *_: (s, 0, 0)),
                pl.BlockSpec(low_table.shape, lambda s, *_: (0, 0)),
                pl.BlockSpec(high_table.shape, lambda s, *_: (0, 0)),
            ],
            out_specs=pl.BlockSpec((blocks, 2 * rows, LANES), lambda s, *_: (0, 0, 0)),
        ),
        out_shape=jax.ShapeDtypeStruct((blocks, 2 * rows, LANES), jnp.float32),
        compiler_params=pltpu.CompilerParams(vmem_limit_bytes=60 * 1024 * 1024),
    )(first, last, gathered, low_table, high_table)

    a = jnp.arange(blocks, dtype=jnp.int32)
    b = jnp.arange(LANES, dtype=jnp.int32)
    first_table = stacked(*phase_table(a, a, blocks))
    cos, sin = phase_table(a, b, GRID)
    scale = 1.0 / math.sqrt(count * devices)
    mu = jnp.concatenate([jnp.arange(0, LANES, 2, dtype=jnp.int32), jnp.arange(1, LANES, 2, dtype=jnp.int32)])
    second_table = stacked(*phase_table(mu, b, LANES))
    whole = lambda shape: pl.BlockSpec(shape, lambda n: (0,) * len(shape))
    picture = pl.pallas_call(
        row_transform_kernel,
        grid=(rows // ROWS_OUT,),
        in_specs=[
            pl.BlockSpec((blocks, 2, ROWS_OUT, LANES), lambda n: (0, 0, n, 0)),
            whole(first_table.shape),
            whole(cos.shape),
            whole(sin.shape),
            whole(second_table.shape),
        ],
        out_specs=pl.BlockSpec((2, ROWS_OUT, blocks, LANES), lambda n: (0, n, 0, 0)),
        out_shape=jax.ShapeDtypeStruct((2, rows, blocks, LANES), jnp.float32),
        compiler_params=pltpu.CompilerParams(vmem_limit_bytes=48 * 1024 * 1024),
    )(plane.reshape(blocks, 2, rows, LANES), first_table, cos * scale, sin * scale, second_table)
    return picture.reshape(2, rows, GRID)


def solution(mesh):
    return jax.shard_map(
        on_device,
        mesh=mesh,
        in_specs=(
            P(None, ("au", "vert")),
            P(None, ("au", "vert")),
            P(None, ("au", "vert")),
            P(("au", "vert"), None),
            P(("au", "vert")),
            P(("au", "vert")),
        ),
        out_specs=P(None, ("au", "vert"), None),
        check_vma=False,
    )
```

profile of v0, /device:TPU:0, one launch (start us, length us, event | category | flops | bytes accessed | tf_op | source)
XLA Modules:
  0.0 407.4 jit_solution(9544527151201993683)
XLA Ops:
  6.5 0.0 all-gather.3.cloned.1.call-start
  6.5 0.8 fusion.158
  7.3 9.7 %all_gather.12 = s32[8192]{0:T(1024)S(1)} all-gather(s32[2048]{0:T(1024)S(1)} %get-tuple-element.82), channel_id=1, replica_groups=mesh['au'=4,'vert'=8] {'au'}, dimensions={0}, use_global_device_ids=true | all-gather | bytes 40960 | tf_op jit(solution)/shard_map/all_gather | solution.py:156
  17.0 9.1 %convert_reduce_fusion = s32[2048]{0:T(1024)S(1)} fusion(s32[2048]{0:T(1024)S(1)} %get-tuple-element.82, s32[8192]{0:T(1024)S(1)} %all_gather.12), kind=kLoop, calls=%fused_computation.1 | loop fusion | flops 50329600 | bytes 49152 | tf_op jit(solution)/shard_map/reduce_sum | solution.py:157
  26.1 1.6 slice_reduce_fusion.15
  27.8 1.6 slice_reduce_fusion.31
  29.4 0.2 fusion.146
  29.6 0.3 fusion.65
  29.9 0.3 fusion.50
  30.3 0.8 concatenate.47
  31.1 12.1 %all_gather.13 = bf16[42,8192]{1,0:T(8,128)(2,1)S(1)} all-gather(bf16[42,2048]{1,0:T(8,128)(2,1)S(1)} %concatenate.47), channel_id=1, replica_groups=mesh['au'=4,'vert'=8] {'au'}, dimensions={1}, use_global_device_ids=true | all-gather | bytes 860160 | tf_op jit(solution)/shard_map/all_gather | solution.py:165
  43.2 0.1 fusion.92
  43.3 17.0 %fusion.2 = bf16[40,2048]{1,0:T(8,128)(2,1)} fusion(s32[8192]{0:T(1024)S(1)} %bitcast.10, bf16[42,8192]{1,0:T(8,128)(2,1)S(1)} %all_gather.13), kind=kOutput, calls=%fused_computation.4 | convolution fusion | flops 1359036416 | bytes 851968 | tf_op jit(solution)/shard_map/dot_general | solution.py:169
  60.3 0.0 all-gather.3.cloned.1.call-update
  60.4 0.1 pad_add_fusion
  60.5 0.1 fusion.104
  60.6 0.2 negate_convert_fusion.2
  60.8 0.1 maximum_maximum_fusion.2.first_ref
  60.9 0.2 sine_multiply_fusion
  61.0 0.6 cosine_convert_fusion
  61.6 0.7 pad_maximum_fusion.low_ref
  62.3 0.3 negate_convert_fusion
  62.7 0.3 negate_convert_fusion.1
  63.0 0.7 maximum_maximum_fusion.high_ref
  63.7 62.4 %all-gather.3.cloned.1.call-done = bf16[1280,2048]{1,0:T(8,128)(2,1)} async-done(((bf16[40,2048]{1,0:T(8,128)(2,1)}), bf16[1280,2048]{1,0:T(8,128)(2,1)}) %all-gather.3.cloned.1.call-update) | async-done | bytes 5242896 | tf_op jit(solution)/shard_map/all_gather | solution.py:170
  126.1 1.4 slice_convert_fusion
  127.5 1.1 fusion.4
  128.7 0.1 fusion.159
  128.8 0.6 and_select_fusion.2.last_ref
  129.4 0.6 and_select_fusion.3.first_ref
  130.0 218.8 %shard_map.64 = f32[64,512,128]{2,1,0:T(8,128)} custom-call(s32[256]{0:T(256)} %and_select_fusion.3.first_ref, s32[256]{0:T(256)} %and_select_fusion.2.last_ref, bf16[32,40,2048]{2,1,0:T(8,128)(2,1)} %bitcast.9, bf16[512,80]{1,0:T(8,128)(2,1)} %pad_maximum_fusion.low_ref, bf16[256,256]{1,0:T(8,128)(2,1)} %maximum_maximum_fusion.high_ref), custom_call_target="tpu_custom_call" | custom-call | tf_op jit(solution)/shard_map/pallas_call | solution.py:186
  348.8 33.5 %shard_map.65 = f32[2,256,64,128]{3,2,1,0:T(8,128)} custom-call(f32[64,2,256,128]{3,2,1,0:T(8,128)} %bitcast.7, bf16[128,128]{1,0:T(8,128)(2,1)S(1)} %maximum_maximum_fusion.2.first_ref, f32[64,128]{1,0:T(8,128)S(1)} %get-tuple-element.116.cos_ref, f32[64,128]{1,0:T(8,128)S(1)} %get-tuple-element.115.sin_ref, ...), custom_call_target="tpu_custom_call" | custom-call | tf_op jit(solution)/shard_map/pallas_call | solution.py:210
  382.4 18.2 %reshape.367 = f32[2,256,8192]{2,1,0:T(8,128)} reshape(f32[2,256,64,128]{3,2,1,0:T(8,128)} %shard_map.65) | data formatting | bytes 33554432 | tf_op jit(solution)/shard_map/reshape | solution.py:224
  (14 shorter events, 0.2 us)
Async XLA Ops:
  6.5 119.6 %all-gather.3.cloned.1.call-start = ((), (), s32[]{:S(2)}) async-start(), calls=%async_computation | async-start | bytes 5406720 | tf_op jit(solution)/shard_map/all_gather | solution.py:170
Sparse Core Ops, SparseCore 0:
  60.5 65.5 all-gather.2
where the time goes:
time: 409 us; the launch traced here: 407 us
  Pallas kernels  252 us (62%)
  waiting for transfers between devices  62.4 us (15%)
  local copies, waits for them, and re-layouts  22.3 us (5%)
  blocking collectives  21.8 us (5%)
  other arithmetic  17.9 us (4%)
  matrix products  17 us (4%)
  between operations  13.6 us (3%)
    pallas_call x1, Pallas kernels, on_device(): pl.pallas_call(functools.partial(tile_spread_kernel, tile=tile, tiles=til...  219 us
    all_gather x1, waiting for transfers between devices, on_device(): gathered = lax.all_gather(payload, ('au', 'vert'), axis=0)  62.4 us
    pallas_call x1, Pallas kernels, on_device(): pl.pallas_call(row_transform_kernel, grid=(rows // ROWS_OUT,), in_specs=[...  33.5 us
    reshape x1, local copies, waits for them, and re-layouts, on_device(): return picture.reshape(2, rows, GRID)  18.2 us
    dot_general x1, matrix products, on_device(): jnp.dot(group[:FIELDS], order, preferred_element_type=jnp.float32)  17 us
    all_gather x1, blocking collectives, on_device(): group = lax.all_gather(payload, 'au', axis=1, tiled=True)  12.1 us
    all_gather x1, blocking collectives, on_device(): keys = lax.all_gather(key, 'au', axis=0, tiled=True)  9.67 us
    reduce_sum x1, other arithmetic, on_device(): rank = jnp.sum((keys[:, None] < key[None, :]).astype(jnp.int32), axis=0)  9.07 us
  transfers between devices with their start and end apart: 1, of which 1 were waited for; matrix products, arithmetic and copies ran while one was open for 1% of the time, Pallas kernels for 0%

commit v1 on v0

v1 whole, which is shorter than its diff:
```python
import functools
import math

import jax
import jax.numpy as jnp
import numpy as np
from jax import lax
from jax.experimental import pallas as pl
from jax.experimental.pallas import tpu as pltpu
from jax.sharding import PartitionSpec as P

GRID = 8192
TAPS = 16
LANES = 128
LOW = 128
FIELDS = 40
WINDOW_BLOCKS = 2
ROWS_OUT = 8
MEBI = 1024 * 1024


def phase_table(left, right, modulus):
    product = left[:, None] * right[None, :] % modulus
    angle = product.astype(jnp.float32) * (2.0 * math.pi / modulus)
    return jnp.cos(angle), jnp.sin(angle)


def rotated(taps, shift):
    tap = jnp.arange(TAPS, dtype=jnp.int32)[:, None]
    turned = jnp.zeros_like(taps)
    for t in range(TAPS):
        turned = turned + jnp.where((shift[None, :] + t) % TAPS == tap, taps[t : t + 1], 0)
    return turned


def spread_tile(fields, low_ref, high_ref, period):
    tile = fields.shape[1]
    taps_u = fields[TAPS : 2 * TAPS]
    extra = fields[2 * TAPS : 2 * TAPS + 8].astype(jnp.float32)
    row_high = extra[3:4].astype(jnp.bfloat16)
    row_mid = extra[4:5]
    row_low = extra[5:6]
    vis_re = extra[6:7].astype(jnp.bfloat16)
    vis_im = extra[7:8].astype(jnp.bfloat16)
    zero = jnp.zeros((), jnp.bfloat16)
    tap = lax.broadcasted_iota(jnp.int32, (TAPS, tile), 0).astype(jnp.float32)
    spot_u = (row_mid + jnp.where(tap < row_low, 1.0, 0.0)).astype(jnp.bfloat16)
    band_u = jnp.concatenate(
        [jnp.where(spot_u == jnp.bfloat16(q), taps_u, zero) for q in range(LOW // TAPS + 1)], axis=0
    )
    high_count = GRID // LOW
    number = lax.broadcasted_iota(jnp.int32, (high_count, tile), 0).astype(jnp.float32).astype(jnp.bfloat16)
    here = number == jnp.broadcast_to(row_high, (high_count, tile))
    picked = jnp.concatenate(
        [
            jnp.where(here, jnp.broadcast_to(vis_re, (high_count, tile)), zero),
            jnp.where(here, jnp.broadcast_to(vis_im, (high_count, tile)), zero),
        ],
        axis=0,
    )
    high = jnp.dot(high_ref[...], picked, preferred_element_type=jnp.float32)
    high_re, high_im = high[:period], high[period:]
    low = jnp.dot(low_ref[...], band_u, preferred_element_type=jnp.float32)
    parts = []
    for begin in range(0, low.shape[0], 2 * period):
        low_re = low[begin : begin + period]
        low_im = low[begin + period : begin + 2 * period]
        parts.append((low_re * high_re - low_im * high_im).astype(jnp.bfloat16))
        parts.append((low_re * high_im + low_im * high_re).astype(jnp.bfloat16))
    return jnp.concatenate(parts, axis=0)


def add_window(spread, fields, block, acc_ref):
    tile = fields.shape[1]
    taps_v = fields[0:TAPS]
    extra = fields[2 * TAPS : 2 * TAPS + 8].astype(jnp.float32)
    tap = lax.broadcasted_iota(jnp.int32, (TAPS, tile), 0).astype(jnp.float32)
    groups = LANES // TAPS
    count = WINDOW_BLOCKS * groups
    zero = jnp.zeros((), jnp.bfloat16)
    spot = (extra[0:1] - block.astype(jnp.float32)) * groups + extra[1:2] + jnp.where(tap < extra[2:3], 1.0, 0.0)
    near = jnp.clip(spot, -1.0, float(count)).astype(jnp.bfloat16)
    band_v = jnp.concatenate([jnp.where(near == jnp.bfloat16(q), taps_v, zero) for q in range(count)], axis=0)
    out = lax.dot_general(spread, band_v, (((1,), (1,)), ((), ())), preferred_element_type=jnp.float32)
    for j in range(WINDOW_BLOCKS):
        acc_ref[block + j] += out[:, j * LANES : (j + 1) * LANES]


def image_kernel(
    first_ref, extra_ref, pay_ref, low_ref, high_ref, one_ref, cos_ref, sin_ref, two_ref, out_ref, acc_ref, *spreads,
    tile, tiles, lists, period,
):
    step = pl.program_id(0)
    group = len(spreads)
    blocks = GRID // LANES

    @pl.when(step == 0)
    def _():
        def clear(n, carry):
            acc_ref[n] = jnp.zeros(acc_ref.shape[1:], jnp.float32)
            return carry

        lax.fori_loop(0, acc_ref.shape[0], clear, 0)

    @pl.when(step < lists)
    def _():
        def some_tiles(g, carry):
            start = g * group
            place = step * tiles + start
            fields = lambda n: pay_ref[0, :, pl.ds(pl.multiple_of((start + n) * tile, tile), tile)]
            for n in range(group):
                spread = spread_tile(fields(n), low_ref, high_ref, period)
                spreads[n][...] = spread
                add_window(spread, fields(n), first_ref[place + n], acc_ref)
            for n in range(group):
                def more(window, carry, n=n):
                    block = jnp.minimum(first_ref[place + n] + window * WINDOW_BLOCKS, blocks)
                    add_window(spreads[n][...], fields(n), block, acc_ref)
                    return carry

                lax.fori_loop(1, extra_ref[place + n], more, 0)
            return carry

        lax.fori_loop(0, tiles // group, some_tiles, 0)

    @pl.when(step >= lists)
    def _():
        first_row = (step - lists) * ROWS_OUT
        at = first_row // period * (2 * period) + first_row % period
        read = lambda part: acc_ref[0:blocks, pl.ds(pl.multiple_of(at + part * period, ROWS_OUT), ROWS_OUT), :]
        planes = [read(0), read(1)]
        stack = jnp.concatenate(
            [jnp.concatenate([plane[:, m, :] for m in range(ROWS_OUT)], axis=1) for plane in planes], axis=0
        ).astype(jnp.bfloat16)
        mid = jnp.dot(one_ref[...], stack, preferred_element_type=jnp.float32)
        cos, sin = cos_ref[...], sin_ref[...]
        rows = []
        for m in range(ROWS_OUT):
            re = mid[:blocks, m * LANES : (m + 1) * LANES]
            im = mid[blocks:, m * LANES : (m + 1) * LANES]
            rows.append(
                jnp.concatenate(
                    [(re * cos - im * sin).astype(jnp.bfloat16), (re * sin + im * cos).astype(jnp.bfloat16)], axis=1
                )
            )
        turned = jnp.concatenate(rows, axis=0)
        out = lax.dot_general(two_ref[...], turned, (((1,), (1,)), ((), ())), preferred_element_type=jnp.float32)
        half = LANES // 2
        left = lax.broadcasted_iota(jnp.int32, (half, LANES), 1) < half
        for part in range(2):
            for pair in range(ROWS_OUT // 2):
                lanes = slice(pair * LANES, (pair + 1) * LANES)
                even = out[2 * part * half : (2 * part + 1) * half, lanes]
                odd = out[(2 * part + 1) * half : (2 * part + 2) * half, lanes]
                out_ref[part, 0, pl.ds(2 * pair, blocks, stride=ROWS_OUT), :] = jnp.where(left, even, pltpu.roll(odd, half, 1))
                out_ref[part, 0, pl.ds(2 * pair + 1, blocks, stride=ROWS_OUT), :] = jnp.where(
                    left, pltpu.roll(even, half, 1), odd
                )

MESH = pl.DeviceIdType.MESH


def exchange_kernel(src_ref, dst_ref, send_sem, recv_sem, *, axis):
    size = send_sem.shape[0]
    me = lax.rem(lax.axis_index(axis), size)
    base = lax.axis_index(axis) - me
    width = src_ref.shape[1] // size
    barrier = pltpu.get_barrier_semaphore()
    for hop in range(1, size):
        peer = base + lax.rem(me + hop, size)
        pl.semaphore_signal(barrier, inc=1, device_id={axis: peer}, device_id_type=MESH)
    pl.semaphore_wait(barrier, size - 1)
    piece = lambda ref, n: ref.at[:, pl.ds(pl.multiple_of(n * width, width), width)]
    copies = []
    for hop in range(1, size):
        peer = lax.rem(me + hop, size)
        copy = pltpu.make_async_remote_copy(
            src_ref=piece(src_ref, peer),
            dst_ref=piece(dst_ref, me),
            send_sem=send_sem.at[hop],
            recv_sem=recv_sem.at[hop],
            device_id={axis: base + peer},
            device_id_type=MESH,
        )
        copy.start()
        copies.append(copy)
    own = pltpu.make_async_copy(piece(src_ref, me), piece(dst_ref, me), send_sem.at[0])
    own.start()
    own.wait()
    for copy in copies:
        copy.wait()


def exchanged(payload, axis, number):
    size = math.gcd(lax.axis_size(axis), payload.shape[1] // LANES)
    return pl.pallas_call(
        functools.partial(exchange_kernel, axis=axis),
        in_specs=[pl.BlockSpec(memory_space=pltpu.HBM)],
        out_specs=pl.BlockSpec(memory_space=pltpu.HBM),
        out_shape=jax.ShapeDtypeStruct(payload.shape, payload.dtype),
        scratch_shapes=[pltpu.SemaphoreType.DMA((size,)), pltpu.SemaphoreType.DMA((size,))],
        compiler_params=pltpu.CompilerParams(collective_id=number, has_side_effects=True),
    )(payload)


def gather_kernel(src_ref, out_ref, own_sem, send_sem, recv_sem):
    n_au, n_vert = lax.axis_size("au"), lax.axis_size("vert")
    a, v = lax.axis_index("au"), lax.axis_index("vert")
    width = out_ref.shape[3]
    inner, cores = math.gcd(n_au, 2), math.gcd(n_vert, 2)
    sizes = {"x": inner, "y": n_au // inner, "z": n_vert // cores, "c": cores}
    place = {"x": lax.rem(a, inner), "y": a // inner, "z": v // cores, "c": lax.rem(v, cores)}

    def at(**moved):
        spot = dict(place)
        for name, hop in moved.items():
            spot[name] = lax.rem(place[name] + hop, sizes[name]) if hop else place[name]
        return spot["y"] * inner + spot["x"], spot["z"] * cores + spot["c"]

    steps = [(name, hop) for name in "xyzc" for hop in range(1, sizes[name])]
    barrier = pltpu.get_barrier_semaphore()
    for name, hop in steps:
        au, vert = at(**{name: hop})
        pl.semaphore_signal(barrier, inc=1, device_id={"au": au, "vert": vert}, device_id_type=MESH)
    pl.semaphore_wait(barrier, len(steps))

    sent = []

    def send(half, source, moved, name, hop):
        au, vert = at(**moved)
        origin = au * n_vert + vert
        to_au, to_vert = at(**{name: hop})
        path = dict(moved)
        path[name] = -hop
        slot = tuple(path.get(n, 0) % sizes[n] for n in "xyzc")
        copy = pltpu.make_async_remote_copy(
            src_ref=source,
            dst_ref=out_ref.at[origin, half],
            send_sem=send_sem.at[len(sent)],
            recv_sem=recv_sem.at[number(half, slot)],
            device_id={"au": to_au, "vert": to_vert},
            device_id_type=MESH,
        )
        copy.start()
        sent.append(copy)

    def number(half, slot):
        total = half
        for n, d in zip("xyzc", slot):
            total = total * sizes[n] + d
        return total

    def arrived(half, moved):
        au, vert = at(**moved)
        block = out_ref.at[au * n_vert + vert, half]
        slot = tuple(moved.get(n, 0) for n in "xyzc")
        pltpu.make_async_copy(block, block, recv_sem.at[number(half, slot)]).wait()
        return block

    order = [("z", "x", "y", "c"), ("z", "y", "x", "c")]

    def pass_on(half, source, moved, stage):
        for name in order[half][stage:]:
            for hop in range(1, sizes[name]):
                send(half, source, moved, name, hop)

    halves = [src_ref.at[:, pl.ds(h * width, width)] for h in range(2)]
    for half in range(2):
        pass_on(half, halves[half], {}, 0)
    origin = a * n_vert + v
    keep = [pltpu.make_async_copy(halves[h], out_ref.at[origin, h], own_sem.at[h]) for h in range(2)]
    for copy in keep:
        copy.start()
    last = []
    for hop_z in range(sizes["z"]):
        for half in range(2):
            if hop_z:
                pass_on(half, arrived(half, {"z": hop_z}), {"z": hop_z}, 1)
        for half in range(2):
            second = order[half][1]
            for hop in range(1, sizes[second]):
                moved = {"z": hop_z, second: hop}
                pass_on(half, arrived(half, moved), moved, 2)
    for hop_z in range(sizes["z"]):
        for half in range(2):
            second, third = order[half][1:3]
            for hop in range(sizes[second]):
                for hop_third in range(1, sizes[third]):
                    moved = {"z": hop_z, second: hop, third: hop_third}
                    pass_on(half, arrived(half, moved), moved, 3)
    for half in range(2):
        for hop in range(1, sizes["c"]):
            for x in range(sizes["x"]):
                for y in range(sizes["y"]):
                    for z in range(sizes["z"]):
                        arrived(half, {"c": hop, "x": x, "y": y, "z": z})
    for copy in keep:
        copy.wait()
    for copy in sent:
        copy.wait_send()


def gathered_everywhere(payload, devices, number):
    fields, count = payload.shape
    return pl.pallas_call(
        gather_kernel,
        in_specs=[pl.BlockSpec(memory_space=pltpu.VMEM)],
        out_specs=pl.BlockSpec(memory_space=pltpu.HBM),
        out_shape=jax.ShapeDtypeStruct((devices, 2, fields, count // 2), payload.dtype),
        scratch_shapes=[
            pltpu.SemaphoreType.DMA((2,)),
            pltpu.SemaphoreType.DMA((2 * devices,)),
            pltpu.SemaphoreType.DMA((2 * devices,)),
        ],
        compiler_params=pltpu.CompilerParams(collective_id=number, has_side_effects=True),
    )(payload)


def fixed_table(left, right, modulus):
    angle = np.outer(left, right) % modulus * (2.0 * math.pi / modulus)
    return np.cos(angle), np.sin(angle)


def stacked(cos, sin):
    return jnp.asarray(np.block([[cos, -sin], [sin, cos]]), dtype=jnp.bfloat16)


def columns_of(payload):
    ends = payload[..., 2 * TAPS : 2 * TAPS + 3, :].astype(jnp.int32)
    return ends[..., 0, :] * LANES + ends[..., 1, :] * TAPS + ends[..., 2, :]


def ordered(payload):
    count = payload.shape[1]
    key = columns_of(payload) * count + jnp.arange(count, dtype=jnp.int32)
    rank = jnp.sum((key[:, None] < key[None, :]).astype(jnp.int32), axis=0)
    order = (rank[:, None] == jnp.arange(count, dtype=jnp.int32)[None, :]).astype(jnp.bfloat16)
    return jnp.dot(payload, order, preferred_element_type=jnp.float32).astype(jnp.bfloat16)


def on_device(visibility, taps_u, taps_v, facet, u_offset, v_offset):
    n_au = lax.axis_size("au")
    n_vert = lax.axis_size("vert")
    devices = n_au * n_vert
    count = visibility.shape[1]
    rows = GRID // devices
    own = lax.axis_index("au") * n_vert + lax.axis_index("vert")
    target = facet[:, 0]
    row = target // n_vert * (GRID // n_au) + u_offset
    col = target % n_vert * (GRID // n_vert) + v_offset
    scalars = jnp.stack(
        [col // LANES, col % LANES // TAPS, col % TAPS, row // LOW, row % LOW // TAPS, row % TAPS]
    ).astype(jnp.bfloat16)
    payload = jnp.concatenate(
        [rotated(taps_v, col % TAPS), rotated(taps_u, row % TAPS), scalars, visibility], axis=0
    )
    payload = ordered(payload)
    payload = exchanged(payload, "vert", 0)
    payload = ordered(payload)
    payload = exchanged(payload, "au", 1)
    payload = ordered(payload)
    lists, count = 2 * devices, count // 2
    gathered = gathered_everywhere(payload, devices, 2).reshape(lists, FIELDS, count)

    tile = math.gcd(count, 256)
    tiles = count // tile
    blocks = GRID // LANES
    columns = columns_of(gathered).reshape(-1, tile)
    first = jnp.min(columns, axis=1) // LANES
    windows = ((jnp.max(columns, axis=1) + TAPS - 1) // LANES - first) // WINDOW_BLOCKS + 1

    k = own * rows + jnp.arange(rows, dtype=jnp.int32)
    high_count = GRID // LOW
    period = min(rows, high_count)
    low_cos, low_sin = phase_table(k, jnp.arange(LOW + TAPS, dtype=jnp.int32), GRID)
    low_table = jnp.concatenate(
        [low_cos.reshape(rows // period, 1, period, -1), low_sin.reshape(rows // period, 1, period, -1)], axis=1
    ).reshape(2 * rows, -1).astype(jnp.bfloat16)
    turns = phase_table(k[:period], jnp.arange(high_count, dtype=jnp.int32), high_count)
    high_table = jnp.block([[turns[0], -turns[1]], [turns[1], turns[0]]]).astype(jnp.bfloat16)

    a, b = np.arange(blocks), np.arange(LANES)
    one_table = stacked(*fixed_table(a, a, blocks))
    cos, sin = fixed_table(a, b, GRID)
    scale = 1.0 / math.sqrt(count * lists)
    mu = np.concatenate([np.arange(0, LANES, 2), np.arange(1, LANES, 2)])
    two_table = stacked(*fixed_table(mu, b, LANES))
    cos, sin = jnp.asarray(cos * scale, dtype=jnp.float32), jnp.asarray(sin * scale, dtype=jnp.float32)
    whole = lambda shape: pl.BlockSpec(shape, lambda n, *_: (0,) * len(shape))
    group = math.gcd(tiles, 4)
    picture = pl.pallas_call(
        functools.partial(image_kernel, tile=tile, tiles=tiles, lists=lists, period=period),
        grid_spec=pltpu.PrefetchScalarGridSpec(
            num_scalar_prefetch=2,
            grid=(lists + rows // ROWS_OUT,),
            in_specs=[
                pl.BlockSpec((1, FIELDS, count), lambda s, *_: (jnp.minimum(s, lists - 1), 0, 0)),
                whole(low_table.shape),
                whole(high_table.shape),
                whole(one_table.shape),
                whole(cos.shape),
                whole(sin.shape),
                whole(two_table.shape),
            ],
            out_specs=pl.BlockSpec(
                (2, 1, blocks * ROWS_OUT, LANES), lambda s, *_: (0, jnp.maximum(s - lists, 0), 0, 0)
            ),
            scratch_shapes=[pltpu.VMEM((blocks + WINDOW_BLOCKS, 2 * rows, LANES), jnp.float32)]
            + [pltpu.VMEM((2 * rows, tile), jnp.bfloat16)] * group,
        ),
        out_shape=jax.ShapeDtypeStruct((2, rows // ROWS_OUT, blocks * ROWS_OUT, LANES), jnp.float32),
        compiler_params=pltpu.CompilerParams(vmem_limit_bytes=56 * MEBI),
    )(first, windows, gathered, low_table, high_table, one_table, cos, sin, two_table)
    picture = picture.reshape(2, rows // ROWS_OUT, blocks, ROWS_OUT, LANES)
    return jnp.transpose(picture, (0, 1, 3, 2, 4)).reshape(2, rows, GRID)


def solution(mesh):
    return jax.shard_map(
        on_device,
        mesh=mesh,
        in_specs=(
            P(None, ("au", "vert")),
            P(None, ("au", "vert")),
            P(None, ("au", "vert")),
            P(("au", "vert"), None),
            P(("au", "vert")),
            P(("au", "vert")),
        ),
        out_specs=P(None, ("au", "vert"), None),
        check_vma=False,
    )
```

time: 409 us -> 194 us (0.47)
  Pallas kernels: 252 us -> 157 us
  waiting for transfers between devices: 62.4 us -> 0 us
  blocking collectives: 21.8 us -> 0 us
  local copies, waits for them, and re-layouts: 22.3 us -> 4.17 us
  between operations: 13.6 us -> 0.19 us
    pallas_call x2 -> x4, Pallas kernels: 252 us -> 157 us  [the longest x1 106 us: on_device(): pl.pallas_call(functools.partial(image_kernel, tile=tile, tiles=tiles, li...]
    all_gather x1 -> x0, waiting for transfers between devices: 62.4 us -> none  [on_device(): gathered = lax.all_gather(payload, ('au', 'vert'), axis=0)]
    all_gather x2 -> x0, blocking collectives: 21.8 us -> none  [the longest x1 12.1 us: on_device(): group = lax.all_gather(payload, 'au', axis=1, tiled=True)]
    reshape x1 -> x0, local copies, waits for them, and re-layouts: 18.2 us -> none  [on_device(): return picture.reshape(2, rows, GRID)]
    reduce_sum x1 -> x3, other arithmetic: 9.07 us -> 5.27 us  [ordered(): rank = jnp.sum((key[:, None] < key[None, :]).astype(jnp.int32), axis=0)]
    dot_general x1 -> x3, matrix products: 17 us -> 14 us  [ordered(): jnp.dot(payload, order, preferred_element_type=jnp.float32)]
  transfers between devices with their start and end apart: 1 -> 0, of which waited for: 1 -> 0; matrix products, arithmetic and copies ran while one was open for 1% -> 0% of each run, Pallas kernels for 0% -> 0%
where the time goes in v1:
time: 194 us; the launch traced here: 190 us
  Pallas kernels  157 us (81%)
  other arithmetic  14.7 us (8%)
  matrix products  14 us (7%)
  local copies, waits for them, and re-layouts  4.17 us (2%)
    pallas_call x1, Pallas kernels, on_device(): pl.pallas_call(functools.partial(image_kernel, tile=tile, tiles=tiles, li...  106 us
    pallas_call x1, Pallas kernels, gathered_everywhere(): pl.pallas_call(gather_kernel, in_specs=[pl.BlockSpec(memory_space=pltpu.V...  36 us
    pallas_call x2, Pallas kernels, exchanged(): pl.pallas_call(functools.partial(exchange_kernel, axis=axis), in_specs=[p...  15.2 us
    dot_general x3, matrix products, ordered(): jnp.dot(payload, order, preferred_element_type=jnp.float32)  14 us
    reduce_sum x3, other arithmetic, ordered(): rank = jnp.sum((key[:, None] < key[None, :]).astype(jnp.int32), axis=0)  5.27 us

profile of v1, /device:TPU:0, one launch (start us, length us, event | category | flops | bytes accessed | tf_op | source)
XLA Modules:
  0.0 190.3 jit_solution(14699754707423914560)
XLA Ops:
  0.0 0.8 fusion.147
  0.8 0.2 negate_convert_fusion
  1.0 0.7 maximum_maximum_fusion.high_ref
  1.7 1.6 slice_reduce_fusion.15
  3.3 1.6 slice_reduce_fusion.31
  5.0 1.3 cosine_convert_fusion
  6.2 0.8 pad_maximum_fusion
  7.0 0.1 fusion.125
  7.1 0.3 fusion.49
  7.4 0.3 fusion.64
  7.8 0.8 concatenate.24
  8.6 0.1 iota_add_fusion.4
  8.7 1.7 convert_reduce_fusion.2
  10.5 4.0 %fusion.8.src_ref = bf16[40,2048]{1,0:T(8,128)(2,1)} fusion(bf16[40,2048]{1,0:T(8,128)(2,1)S(1)} %concatenate.24, s32[2048]{0:T(1024)S(1)} %convert_reduce_fusion.2), kind=kOutput, calls=%fused_computation.14 | convolution fusion | flops 339820544 | bytes 335872 | tf_op jit(solution)/shard_map/dot_general | solution.py:338
  14.5 9.2 %shard_map.100 = bf16[40,2048]{1,0:T(8,128)(2,1)} custom-call(bf16[40,2048]{1,0:T(8,128)(2,1)} %fusion.8.src_ref), custom_call_target="tpu_custom_call" | custom-call | tf_op jit(solution)/shard_map/pallas_call | solution.py:196
  23.7 0.8 slice_convert_fusion.2
  24.5 1.7 convert_reduce_fusion.1
  26.2 5.0 %fusion.7.src_ref = bf16[40,2048]{1,0:T(8,128)(2,1)} fusion(bf16[40,2048]{1,0:T(8,128)(2,1)} %shard_map.100, s32[2048]{0:T(1024)S(1)} %convert_reduce_fusion.1), kind=kOutput, calls=%fused_computation.13 | convolution fusion | flops 339820544 | bytes 335872 | tf_op jit(solution)/shard_map/dot_general | solution.py:338
  31.2 6.0 %shard_map.101 = bf16[40,2048]{1,0:T(8,128)(2,1)} custom-call(bf16[40,2048]{1,0:T(8,128)(2,1)} %fusion.7.src_ref), custom_call_target="tpu_custom_call" | custom-call | tf_op jit(solution)/shard_map/pallas_call | solution.py:196
  37.2 0.8 slice_convert_fusion.1
  38.0 1.9 convert_reduce_fusion
  39.9 5.0 %fusion.6.src_ref = bf16[40,2048]{1,0:T(8,128)(2,1)} fusion(bf16[40,2048]{1,0:T(8,128)(2,1)} %shard_map.101, s32[2048]{0:T(1024)S(1)} %convert_reduce_fusion), kind=kOutput, calls=%fused_computation.12 | convolution fusion | flops 339820544 | bytes 335872 | tf_op jit(solution)/shard_map/dot_general | solution.py:338
  44.8 36.0 %shard_map.102 = bf16[32,2,40,1024]{3,2,1,0:T(8,128)(2,1)} custom-call(bf16[40,2048]{1,0:T(8,128)(2,1)} %fusion.6.src_ref), custom_call_target="tpu_custom_call" | custom-call | tf_op jit(solution)/shard_map/pallas_call | solution.py:305
  80.9 1.4 slice_convert_fusion
  82.3 1.1 fusion.12
  83.4 0.1 add.670
  83.5 0.1 fusion.148
  83.6 0.6 fusion.145
  84.2 106.1 %shard_map.103 = f32[2,32,512,128]{3,2,1,0:T(8,128)} custom-call(s32[256]{0:T(256)} %get-tuple-element.40.first_ref, s32[256]{0:T(256)} %get-tuple-element.39.extra_ref, bf16[64,40,1024]{2,1,0:T(8,128)(2,1)} %bitcast.18, bf16[512,144]{1,0:T(8,128)(2,1)} %bitcast.19, bf16[128,128]{1,0:T(8,128)(2,1)} %maximum_maximum_fusion.high_ref, ...), custom_call_target="tpu_custom_call" | custom-call | tf_op jit(solution)/shard_map/pallas_call | solution.py:391
  (14 shorter events, 0.1 us)

commit v2 on v1

--- a/solution.py
+++ b/solution.py
@@ -16,6 +16,8 @@
 FIELDS = 40
 WINDOW_BLOCKS = 2
 ROWS_OUT = 8
+OUT_GROUPS = 2
+PAD = 8
 MEBI = 1024 * 1024
 
 
@@ -82,8 +84,10 @@
     near = jnp.clip(spot, -1.0, float(count)).astype(jnp.bfloat16)
     band_v = jnp.concatenate([jnp.where(near == jnp.bfloat16(q), taps_v, zero) for q in range(count)], axis=0)
     out = lax.dot_general(spread, band_v, (((1,), (1,)), ((), ())), preferred_element_type=jnp.float32)
+    pitch = spread.shape[0] + PAD
     for j in range(WINDOW_BLOCKS):
-        acc_ref[block + j] += out[:, j * LANES : (j + 1) * LANES]
+        rows = pl.ds(pl.multiple_of((block + j) * pitch, PAD), spread.shape[0])
+        acc_ref[rows, :] += out[:, j * LANES : (j + 1) * LANES]
 
 
 def image_kernel(
@@ -91,28 +95,28 @@
     tile, tiles, lists, period,
 ):
     step = pl.program_id(0)
-    group = len(spreads)
     blocks = GRID // LANES
+    pitch = low_ref.shape[0] + PAD
 
     @pl.when(step == 0)
     def _():
         def clear(n, carry):
-            acc_ref[n] = jnp.zeros(acc_ref.shape[1:], jnp.float32)
+            rows = pl.ds(pl.multiple_of(n * pitch, PAD), pitch)
+            acc_ref[rows, :] = jnp.zeros((pitch, LANES), jnp.float32)
             return carry
 
-        lax.fori_loop(0, acc_ref.shape[0], clear, 0)
+        lax.fori_loop(0, acc_ref.shape[0] // pitch, clear, 0)
 
     @pl.when(step < lists)
     def _():
-        def some_tiles(g, carry):
-            start = g * group
-            place = step * tiles + start
-            fields = lambda n: pay_ref[0, :, pl.ds(pl.multiple_of((start + n) * tile, tile), tile)]
-            for n in range(group):
+        def one_list(part, carry):
+            place = (step * pay_ref.shape[0] + part) * 2 * tiles
+            fields = lambda n: pay_ref[part, n // tiles, :, n % tiles * tile : (n % tiles + 1) * tile]
+            for n in range(2 * tiles):
                 spread = spread_tile(fields(n), low_ref, high_ref, period)
                 spreads[n][...] = spread
                 add_window(spread, fields(n), first_ref[place + n], acc_ref)
-            for n in range(group):
+            for n in range(2 * tiles):
                 def more(window, carry, n=n):
                     block = jnp.minimum(first_ref[place + n] + window * WINDOW_BLOCKS, blocks)
                     add_window(spreads[n][...], fields(n), block, acc_ref)
@@ -121,65 +125,87 @@
                 lax.fori_loop(1, extra_ref[place + n], more, 0)
             return carry
 
-        lax.fori_loop(0, tiles // group, some_tiles, 0)
+        lax.fori_loop(0, pay_ref.shape[0], one_list, 0)
 
     @pl.when(step >= lists)
     def _():
-        first_row = (step - lists) * ROWS_OUT
-        at = first_row // period * (2 * period) + first_row % period
-        read = lambda part: acc_ref[0:blocks, pl.ds(pl.multiple_of(at + part * period, ROWS_OUT), ROWS_OUT), :]
-        planes = [read(0), read(1)]
-        stack = jnp.concatenate(
-            [jnp.concatenate([plane[:, m, :] for m in range(ROWS_OUT)], axis=1) for plane in planes], axis=0
-        ).astype(jnp.bfloat16)
-        mid = jnp.dot(one_ref[...], stack, preferred_element_type=jnp.float32)
-        cos, sin = cos_ref[...], sin_ref[...]
-        rows = []
-        for m in range(ROWS_OUT):
-            re = mid[:blocks, m * LANES : (m + 1) * LANES]
-            im = mid[blocks:, m * LANES : (m + 1) * LANES]
-            rows.append(
-                jnp.concatenate(
-                    [(re * cos - im * sin).astype(jnp.bfloat16), (re * sin + im * cos).astype(jnp.bfloat16)], axis=1
-                )
+        def some_rows(turn, carry):
+            for group in range(OUT_GROUPS):
+                here = turn * OUT_GROUPS + group
+                first_row = ((step - lists) * out_ref.shape[1] + here) * ROWS_OUT
+                at = first_row // period * (2 * period) + first_row % period
+                image_rows(at, period, acc_ref, one_ref, cos_ref, sin_ref, two_ref, out_ref, here, pitch)
+            return carry
+
+        lax.fori_loop(0, out_ref.shape[1] // OUT_GROUPS, some_rows, 0)
+
+
+def image_rows(at, period, acc_ref, one_ref, cos_ref, sin_ref, two_ref, out_ref, group, pitch):
+    blocks = GRID // LANES
+    row = lambda part, m: acc_ref[pl.ds(at + part * period + m, blocks, stride=pitch), :].astype(jnp.bfloat16)
+    stack = jnp.concatenate(
+        [jnp.concatenate([row(part, m) for m in range(ROWS_OUT)], axis=1) for part in range(2)], axis=0
+    )
+    mid = jnp.dot(one_ref[...], stack, preferred_element_type=jnp.float32)
+    cos, sin = cos_ref[...], sin_ref[...]
+    rows = []
+    for m in range(ROWS_OUT):
+        re = mid[:blocks, m * LANES : (m + 1) * LANES]
+        im = mid[blocks:, m * LANES : (m + 1) * LANES]
+        rows.append(
+            jnp.concatenate(
+                [(re * cos - im * sin).astype(jnp.bfloat16), (re * sin + im * cos).astype(jnp.bfloat16)], axis=1
             )
-        turned = jnp.concatenate(rows, axis=0)
-        out = lax.dot_general(two_ref[...], turned, (((1,), (1,)), ((), ())), preferred_element_type=jnp.float32)
-        half = LANES // 2
-        left = lax.broadcasted_iota(jnp.int32, (half, LANES), 1) < half
-        for part in range(2):
-            for pair in range(ROWS_OUT // 2):
-                lanes = slice(pair * LANES, (pair + 1) * LANES)
-                even = out[2 * part * half : (2 * part + 1) * half, lanes]
-                odd = out[(2 * part + 1) * half : (2 * part + 2) * half, lanes]
-                out_ref[part, 0, pl.ds(2 * pair, blocks, stride=ROWS_OUT), :] = jnp.where(left, even, pltpu.roll(odd, half, 1))
-                out_ref[part, 0, pl.ds(2 * pair + 1, blocks, stride=ROWS_OUT), :] = jnp.where(
-                    left, pltpu.roll(even, half, 1), odd
-                )
+        )
+    turned = jnp.concatenate(rows, axis=0)
+    out = lax.dot_general(two_ref[...], turned, (((1,), (1,)), ((), ())), preferred_element_type=jnp.float32)
+    half = LANES // 2
+    left = lax.broadcasted_iota(jnp.int32, (half, LANES), 1) < half
+    for part in range(2):
+        for pair in range(ROWS_OUT // 2):
+            lanes = slice(pair * LANES, (pair + 1) * LANES)
+            even = out[2 * part * half : (2 * part + 1) * half, lanes]
+            odd = out[(2 * part + 1) * half : (2 * part + 2) * half, lanes]
+            put = lambda m: pl.ds(m, blocks, stride=ROWS_OUT)
+            out_ref[part, group, put(2 * pair), :] = jnp.where(left, even, pltpu.roll(odd, half, 1))
+            out_ref[part, group, put(2 * pair + 1), :] = jnp.where(left, pltpu.roll(even, half, 1), odd)
+
 
 MESH = pl.DeviceIdType.MESH
 
 
-def exchange_kernel(src_ref, dst_ref, send_sem, recv_sem, *, axis):
-    size = send_sem.shape[0]
-    me = lax.rem(lax.axis_index(axis), size)
-    base = lax.axis_index(axis) - me
-    width = src_ref.shape[1] // size
+def exchange_kernel(src_ref, dst_ref, send_sem, recv_sem, *, sizes):
+    spot, near, me = {}, {}, 0
+    for axis, size in sizes.items():
+        near[axis] = lax.rem(lax.axis_index(axis), size)
+        spot[axis] = lax.axis_index(axis) - near[axis]
+        me = me * size + near[axis]
+    total = math.prod(sizes.values())
+    width = src_ref.shape[1] // total
+
+    def peer(hop):
+        index, device = 0, {}
+        for place, (axis, size) in enumerate(sizes.items()):
+            step = hop // math.prod(list(sizes.values())[place + 1 :]) % size
+            digit = lax.rem(near[axis] + step, size) if step else near[axis]
+            index = index * size + digit
+            device[axis] = spot[axis] + digit
+        return index, device
+
     barrier = pltpu.get_barrier_semaphore()
-    for hop in range(1, size):
-        peer = base + lax.rem(me + hop, size)
-        pl.semaphore_signal(barrier, inc=1, device_id={axis: peer}, device_id_type=MESH)
-    pl.semaphore_wait(barrier, size - 1)
+    for hop in range(1, total):
+        pl.semaphore_signal(barrier, inc=1, device_id=peer(hop)[1], device_id_type=MESH)
+    pl.semaphore_wait(barrier, total - 1)
     piece = lambda ref, n: ref.at[:, pl.ds(pl.multiple_of(n * width, width), width)]
     copies = []
-    for hop in range(1, size):
-        peer = lax.rem(me + hop, size)
+    for hop in range(1, total):
+        index, device = peer(hop)
         copy = pltpu.make_async_remote_copy(
-            src_ref=piece(src_ref, peer),
+            src_ref=piece(src_ref, index),
             dst_ref=piece(dst_ref, me),
             send_sem=send_sem.at[hop],
             recv_sem=recv_sem.at[hop],
-            device_id={axis: base + peer},
+            device_id=device,
             device_id_type=MESH,
         )
         copy.start()
@@ -191,14 +217,16 @@
         copy.wait()
 
 
-def exchanged(payload, axis, number):
-    size = math.gcd(lax.axis_size(axis), payload.shape[1] // LANES)
+def exchanged(payload, number):
+    vert = math.gcd(lax.axis_size("vert"), payload.shape[1] // LANES)
+    sizes = {"au": math.gcd(lax.axis_size("au"), payload.shape[1] // LANES // vert), "vert": vert}
+    total = math.prod(sizes.values())
     return pl.pallas_call(
-        functools.partial(exchange_kernel, axis=axis),
+        functools.partial(exchange_kernel, sizes=sizes),
         in_specs=[pl.BlockSpec(memory_space=pltpu.HBM)],
         out_specs=pl.BlockSpec(memory_space=pltpu.HBM),
         out_shape=jax.ShapeDtypeStruct(payload.shape, payload.dtype),
-        scratch_shapes=[pltpu.SemaphoreType.DMA((size,)), pltpu.SemaphoreType.DMA((size,))],
+        scratch_shapes=[pltpu.SemaphoreType.DMA((total,)), pltpu.SemaphoreType.DMA((total,))],
         compiler_params=pltpu.CompilerParams(collective_id=number, has_side_effects=True),
     )(payload)
 
@@ -355,15 +383,11 @@
         [rotated(taps_v, col % TAPS), rotated(taps_u, row % TAPS), scalars, visibility], axis=0
     )
     payload = ordered(payload)
-    payload = exchanged(payload, "vert", 0)
+    payload = exchanged(payload, 0)
     payload = ordered(payload)
-    payload = exchanged(payload, "au", 1)
-    payload = ordered(payload)
-    lists, count = 2 * devices, count // 2
-    gathered = gathered_everywhere(payload, devices, 2).reshape(lists, FIELDS, count)
-
-    tile = math.gcd(count, 256)
-    tiles = count // tile
+    gathered = gathered_everywhere(payload, devices, 1)
+    tile = math.gcd(count // 2, 256)
+    tiles = count // 2 // tile
     blocks = GRID // LANES
     columns = columns_of(gathered).reshape(-1, tile)
     first = jnp.min(columns, axis=1) // LANES
@@ -382,19 +406,21 @@
     a, b = np.arange(blocks), np.arange(LANES)
     one_table = stacked(*fixed_table(a, a, blocks))
     cos, sin = fixed_table(a, b, GRID)
-    scale = 1.0 / math.sqrt(count * lists)
+    scale = 1.0 / math.sqrt(count * devices)
     mu = np.concatenate([np.arange(0, LANES, 2), np.arange(1, LANES, 2)])
     two_table = stacked(*fixed_table(mu, b, LANES))
     cos, sin = jnp.asarray(cos * scale, dtype=jnp.float32), jnp.asarray(sin * scale, dtype=jnp.float32)
+    together = math.gcd(devices, 4)
+    steps = devices // together
+    out_rows = OUT_GROUPS * math.gcd(rows // (ROWS_OUT * OUT_GROUPS), 2)
     whole = lambda shape: pl.BlockSpec(shape, lambda n, *_: (0,) * len(shape))
-    group = math.gcd(tiles, 4)
     picture = pl.pallas_call(
-        functools.partial(image_kernel, tile=tile, tiles=tiles, lists=lists, period=period),
+        functools.partial(image_kernel, tile=tile, tiles=tiles, lists=steps, period=period),
         grid_spec=pltpu.PrefetchScalarGridSpec(
             num_scalar_prefetch=2,
-            grid=(lists + rows // ROWS_OUT,),
+            grid=(steps + rows // (ROWS_OUT * out_rows),),
             in_specs=[
-                pl.BlockSpec((1, FIELDS, count), lambda s, *_: (jnp.minimum(s, lists - 1), 0, 0)),
+                pl.BlockSpec((together, 2, FIELDS, count // 2), lambda s, *_: (jnp.minimum(s, steps - 1), 0, 0, 0)),
                 whole(low_table.shape),
                 whole(high_table.shape),
                 whole(one_table.shape),
@@ -403,10 +429,10 @@
                 whole(two_table.shape),
             ],
             out_specs=pl.BlockSpec(
-                (2, 1, blocks * ROWS_OUT, LANES), lambda s, *_: (0, jnp.maximum(s - lists, 0), 0, 0)
+                (2, out_rows, blocks * ROWS_OUT, LANES), lambda s, *_: (0, jnp.maximum(s - steps, 0), 0, 0)
             ),
-            scratch_shapes=[pltpu.VMEM((blocks + WINDOW_BLOCKS, 2 * rows, LANES), jnp.float32)]
-            + [pltpu.VMEM((2 * rows, tile), jnp.bfloat16)] * group,
+            scratch_shapes=[pltpu.VMEM(((blocks + WINDOW_BLOCKS) * (2 * rows + PAD), LANES), jnp.float32)]
+            + [pltpu.VMEM((2 * rows, tile), jnp.bfloat16)] * (2 * tiles),
         ),
         out_shape=jax.ShapeDtypeStruct((2, rows // ROWS_OUT, blocks * ROWS_OUT, LANES), jnp.float32),
         compiler_params=pltpu.CompilerParams(vmem_limit_bytes=56 * MEBI),

time: 194 us -> 179 us (0.923)
  the two profiles are of different devices: /device:TPU:0 before, /device:TPU:9 now
where the time goes in v2:
time: 179 us
  Pallas kernels  153 us (85%)
  other arithmetic  12.1 us (7%)
  matrix products  9.01 us (5%)
  local copies, waits for them, and re-layouts  4.3 us (2%)
    pallas_call x1, Pallas kernels, on_device(): pl.pallas_call(functools.partial(image_kernel, tile=tile, tiles=tiles, li...  102 us
    pallas_call x1, Pallas kernels, gathered_everywhere(): pl.pallas_call(gather_kernel, in_specs=[pl.BlockSpec(memory_space=pltpu.V...  41.8 us
    pallas_call x1, Pallas kernels, exchanged(): pl.pallas_call(functools.partial(exchange_kernel, sizes=sizes), in_specs=...  9.3 us
    dot_general x2, matrix products, ordered(): jnp.dot(payload, order, preferred_element_type=jnp.float32)  9.01 us

profile of v2, /device:TPU:9, one launch (start us, length us, event | category | flops | bytes accessed | tf_op | source)
XLA Modules:
  0.0 178.8 jit_solution(9176358687889621133)
XLA Ops:
  0.0 0.8 fusion.142
  0.8 0.2 negate_convert_fusion
  1.0 0.7 maximum_maximum_fusion.high_ref
  1.7 1.6 slice_reduce_fusion.15
  3.3 1.6 slice_reduce_fusion.31
  5.0 1.3 cosine_convert_fusion
  6.2 0.8 pad_maximum_fusion
  7.0 0.1 fusion.122
  7.1 0.3 fusion.46
  7.4 0.3 fusion.61
  7.8 0.8 concatenate.24
  8.6 0.1 iota_add_fusion.2
  8.7 1.7 convert_reduce_fusion.1
  10.5 4.0 %fusion.5.src_ref = bf16[40,2048]{1,0:T(8,128)(2,1)} fusion(bf16[40,2048]{1,0:T(8,128)(2,1)S(1)} %concatenate.24, s32[2048]{0:T(1024)S(1)} %convert_reduce_fusion.1), kind=kOutput, calls=%fused_computation.9 | convolution fusion | flops 339820544 | bytes 335872 | tf_op jit(solution)/shard_map/dot_general | solution.py:366
  14.5 9.3 %shard_map.100 = bf16[40,2048]{1,0:T(8,128)(2,1)} custom-call(bf16[40,2048]{1,0:T(8,128)(2,1)} %fusion.5.src_ref), custom_call_target="tpu_custom_call" | custom-call | tf_op jit(solution)/shard_map/pallas_call | solution.py:224
  23.8 0.8 slice_convert_fusion.1
  24.6 1.7 convert_reduce_fusion
  26.3 5.0 %fusion.4.src_ref = bf16[40,2048]{1,0:T(8,128)(2,1)} fusion(bf16[40,2048]{1,0:T(8,128)(2,1)} %shard_map.100, s32[2048]{0:T(1024)S(1)} %convert_reduce_fusion), kind=kOutput, calls=%fused_computation.8 | convolution fusion | flops 339820544 | bytes 335872 | tf_op jit(solution)/shard_map/dot_general | solution.py:366
  31.3 41.8 %shard_map.101.pay_ref = bf16[32,2,40,1024]{3,2,1,0:T(8,128)(2,1)} custom-call(bf16[40,2048]{1,0:T(8,128)(2,1)} %fusion.4.src_ref), custom_call_target="tpu_custom_call" | custom-call | tf_op jit(solution)/shard_map/pallas_call | solution.py:333
  73.1 1.4 slice_convert_fusion
  74.5 1.2 fusion.9
  75.7 0.2 add.638
  76.0 0.1 fusion.143
  76.1 0.6 fusion.140
  76.7 102.1 %shard_map.102 = f32[2,32,512,128]{3,2,1,0:T(8,128)} custom-call(s32[256]{0:T(256)} %get-tuple-element.40.first_ref, s32[256]{0:T(256)} %get-tuple-element.39.extra_ref, bf16[32,2,40,1024]{3,2,1,0:T(8,128)(2,1)} %shard_map.101.pay_ref, bf16[512,144]{1,0:T(8,128)(2,1)} %bitcast.13, bf16[128,128]{1,0:T(8,128)(2,1)} %maximum_maximum_fusion.high_ref, ...), custom_call_target="tpu_custom_call" | custom-call | tf_op jit(solution)/shard_map/pallas_call | solution.py:417
  (12 shorter events, 0.1 us)

commit v3 on v2

--- a/solution.py
+++ b/solution.py
@@ -217,9 +217,8 @@
         copy.wait()
 
 
-def exchanged(payload, number):
-    vert = math.gcd(lax.axis_size("vert"), payload.shape[1] // LANES)
-    sizes = {"au": math.gcd(lax.axis_size("au"), payload.shape[1] // LANES // vert), "vert": vert}
+def exchanged(payload, axis, number):
+    sizes = {axis: math.gcd(lax.axis_size(axis), payload.shape[1] // LANES)}
     total = math.prod(sizes.values())
     return pl.pallas_call(
         functools.partial(exchange_kernel, sizes=sizes),
@@ -231,6 +230,15 @@
     )(payload)
 
 
+def flipped(place, mask):
+    bit = 1
+    while bit <= mask:
+        if mask & bit:
+            place = place + bit - 2 * bit * lax.rem(place // bit, 2)
+        bit *= 2
+    return place
+
+
 def gather_kernel(src_ref, out_ref, own_sem, send_sem, recv_sem):
     n_au, n_vert = lax.axis_size("au"), lax.axis_size("vert")
     a, v = lax.axis_index("au"), lax.axis_index("vert")
@@ -242,7 +250,7 @@
     def at(**moved):
         spot = dict(place)
         for name, hop in moved.items():
-            spot[name] = lax.rem(place[name] + hop, sizes[name]) if hop else place[name]
+            spot[name] = flipped(place[name], hop)
         return spot["y"] * inner + spot["x"], spot["z"] * cores + spot["c"]
 
     steps = [(name, hop) for name in "xyzc" for hop in range(1, sizes[name])]
@@ -259,8 +267,8 @@
         origin = au * n_vert + vert
         to_au, to_vert = at(**{name: hop})
         path = dict(moved)
-        path[name] = -hop
-        slot = tuple(path.get(n, 0) % sizes[n] for n in "xyzc")
+        path[name] = hop
+        slot = tuple(path.get(n, 0) for n in "xyzc")
         copy = pltpu.make_async_remote_copy(
             src_ref=source,
             dst_ref=out_ref.at[origin, half],
@@ -299,16 +307,23 @@
     keep = [pltpu.make_async_copy(halves[h], out_ref.at[origin, h], own_sem.at[h]) for h in range(2)]
     for copy in keep:
         copy.start()
-    last = []
-    for hop_z in range(sizes["z"]):
+
+    def along_z(hop_z):
         for half in range(2):
-            if hop_z:
-                pass_on(half, arrived(half, {"z": hop_z}), {"z": hop_z}, 1)
+            pass_on(half, arrived(half, {"z": hop_z}), {"z": hop_z}, 1)
+
+    def along_second(hop_z):
         for half in range(2):
             second = order[half][1]
             for hop in range(1, sizes[second]):
                 moved = {"z": hop_z, second: hop}
                 pass_on(half, arrived(half, moved), moved, 2)
+
+    for hop_z in range(sizes["z"] + 1):
+        if 0 < hop_z < sizes["z"]:
+            along_z(hop_z)
+        if hop_z != 1:
+            along_second(max(hop_z - 1, 0))
     for hop_z in range(sizes["z"]):
         for half in range(2):
             second, third = order[half][1:3]
@@ -383,9 +398,11 @@
         [rotated(taps_v, col % TAPS), rotated(taps_u, row % TAPS), scalars, visibility], axis=0
     )
     payload = ordered(payload)
-    payload = exchanged(payload, 0)
+    payload = exchanged(payload, "vert", 0)
     payload = ordered(payload)
-    gathered = gathered_everywhere(payload, devices, 1)
+    payload = exchanged(payload, "au", 1)
+    payload = ordered(payload)
+    gathered = gathered_everywhere(payload, devices, 2)
     tile = math.gcd(count // 2, 256)
     tiles = count // 2 // tile
     blocks = GRID // LANES

time: 179 us -> 172 us (0.961)
  the two profiles are of different devices: /device:TPU:9 before, /device:TPU:0 now
where the time goes in v3:
time: 172 us; the launch traced here: 169 us
  Pallas kernels  136 us (79%)
  other arithmetic  14.8 us (9%)
  matrix products  14 us (8%)
  local copies, waits for them, and re-layouts  4.3 us (2%)
    pallas_call x1, Pallas kernels, on_device(): pl.pallas_call(functools.partial(image_kernel, tile=tile, tiles=tiles, li...  88.3 us
    pallas_call x1, Pallas kernels, gathered_everywhere(): pl.pallas_call(gather_kernel, in_specs=[pl.BlockSpec(memory_space=pltpu.V...  32.6 us
    pallas_call x2, Pallas kernels, exchanged(): pl.pallas_call(functools.partial(exchange_kernel, sizes=sizes), in_specs=...  15.2 us
    dot_general x3, matrix products, ordered(): jnp.dot(payload, order, preferred_element_type=jnp.float32)  14 us
    reduce_sum x3, other arithmetic, ordered(): rank = jnp.sum((key[:, None] < key[None, :]).astype(jnp.int32), axis=0)  5.27 us

profile of v3, /device:TPU:0, one launch (start us, length us, event | category | flops | bytes accessed | tf_op | source)
XLA Modules:
  0.0 169.3 jit_solution(2402607606227589381)
XLA Ops:
  0.0 0.8 fusion.147
  0.8 0.2 negate_convert_fusion
  1.0 0.7 maximum_maximum_fusion.high_ref
  1.7 1.6 slice_reduce_fusion.15
  3.3 1.6 slice_reduce_fusion.31
  5.0 1.3 cosine_convert_fusion
  6.2 0.8 pad_maximum_fusion
  7.0 0.1 fusion.125
  7.1 0.3 fusion.49
  7.4 0.3 fusion.64
  7.8 0.8 concatenate.24
  8.6 0.1 iota_add_fusion.4
  8.7 1.7 %convert_reduce_fusion.2 = s32[2048]{0:T(1024)S(1)} fusion(s32[2048]{0:T(1024)S(1)} %bitcast.20, s32[2048]{0:T(1024)S(1)} %iota_add_fusion.5), kind=kLoop, calls=%fused_computation.5 | loop fusion | flops 12580864 | bytes 24576 | tf_op jit(solution)/shard_map/reduce_sum | solution.py:379
  10.5 4.0 %fusion.8.src_ref = bf16[40,2048]{1,0:T(8,128)(2,1)} fusion(bf16[40,2048]{1,0:T(8,128)(2,1)S(1)} %concatenate.24, s32[2048]{0:T(1024)S(1)} %convert_reduce_fusion.2), kind=kOutput, calls=%fused_computation.14 | convolution fusion | flops 339820544 | bytes 335872 | tf_op jit(solution)/shard_map/dot_general | solution.py:381
  14.5 9.2 %shard_map.100 = bf16[40,2048]{1,0:T(8,128)(2,1)} custom-call(bf16[40,2048]{1,0:T(8,128)(2,1)} %fusion.8.src_ref), custom_call_target="tpu_custom_call" | custom-call | tf_op jit(solution)/shard_map/pallas_call | solution.py:223
  23.7 0.8 slice_convert_fusion.2
  24.5 1.7 %convert_reduce_fusion.1 = s32[2048]{0:T(1024)S(1)} fusion(s32[2048]{0:T(1024)S(1)} %bitcast.21, s32[2048]{0:T(1024)S(1)} %iota_add_fusion.3), kind=kLoop, calls=%fused_computation.3 | loop fusion | flops 12580864 | bytes 24576 | tf_op jit(solution)/shard_map/reduce_sum | solution.py:379
  26.2 5.0 %fusion.7.src_ref = bf16[40,2048]{1,0:T(8,128)(2,1)} fusion(bf16[40,2048]{1,0:T(8,128)(2,1)} %shard_map.100, s32[2048]{0:T(1024)S(1)} %convert_reduce_fusion.1), kind=kOutput, calls=%fused_computation.13 | convolution fusion | flops 339820544 | bytes 335872 | tf_op jit(solution)/shard_map/dot_general | solution.py:381
  31.2 6.0 %shard_map.101 = bf16[40,2048]{1,0:T(8,128)(2,1)} custom-call(bf16[40,2048]{1,0:T(8,128)(2,1)} %fusion.7.src_ref), custom_call_target="tpu_custom_call" | custom-call | tf_op jit(solution)/shard_map/pallas_call | solution.py:223
  37.2 0.8 slice_convert_fusion.1
  38.0 1.9 %convert_reduce_fusion = s32[2048]{0:T(1024)S(1)} fusion(s32[2048]{0:T(1024)S(1)} %bitcast.22, s32[2048]{0:T(1024)S(1)} %iota_add_fusion.1), kind=kLoop, calls=%fused_computation.1 | loop fusion | flops 12580864 | bytes 24576 | tf_op jit(solution)/shard_map/reduce_sum | solution.py:379
  39.9 5.0 %fusion.6.src_ref = bf16[40,2048]{1,0:T(8,128)(2,1)} fusion(bf16[40,2048]{1,0:T(8,128)(2,1)} %shard_map.101, s32[2048]{0:T(1024)S(1)} %convert_reduce_fusion), kind=kOutput, calls=%fused_computation.12 | convolution fusion | flops 339820544 | bytes 335872 | tf_op jit(solution)/shard_map/dot_general | solution.py:381
  44.8 32.6 %shard_map.102.pay_ref = bf16[32,2,40,1024]{3,2,1,0:T(8,128)(2,1)} custom-call(bf16[40,2048]{1,0:T(8,128)(2,1)} %fusion.6.src_ref), custom_call_target="tpu_custom_call" | custom-call | tf_op jit(solution)/shard_map/pallas_call | solution.py:348
  77.4 1.4 slice_convert_fusion
  78.8 1.2 fusion.12
  80.1 0.2 add.670
  80.3 0.1 fusion.148
  80.5 0.6 fusion.145
  81.0 88.3 %shard_map.103 = f32[2,32,512,128]{3,2,1,0:T(8,128)} custom-call(s32[256]{0:T(256)} %get-tuple-element.40.first_ref, s32[256]{0:T(256)} %get-tuple-element.39.extra_ref, bf16[32,2,40,1024]{3,2,1,0:T(8,128)(2,1)} %shard_map.102.pay_ref, bf16[512,144]{1,0:T(8,128)(2,1)} %bitcast.16, bf16[128,128]{1,0:T(8,128)(2,1)} %maximum_maximum_fusion.high_ref, ...), custom_call_target="tpu_custom_call" | custom-call | tf_op jit(solution)/shard_map/pallas_call | solution.py:434
  (14 shorter events, 0.1 us)
